TPU v7x, 32 devices: a whole 2x2x4 slice. The times are simulated.
32 devices in a mesh: row: 4 (over z), col: 8 (over y, x, core).
Axes of the slice: x: 2, y: 2, z: 4, core: 2. Of those that a mesh axis runs over, the one named last changes fastest.
Arguments:
- diag_blocks: float32 [8, 16, 512, 512], P('row', 'col'), may hold values from -4 to 16, as said below
- horizontal: bfloat16 [8, 16, 512, 512], P('row', 'col'), may hold values from -0.125 to 0.125
- vertical: bfloat16 [8, 16, 512, 512], P('row', 'col'), may hold values from -0.125 to 0.125
Outputs:
- red_factor: float32 [8, 8, 512, 512], P('row', 'col')
- black_schur: float32 [8, 8, 512, 512], P('row', 'col')
- black_links: bfloat16 [8, 8, 4, 512, 512], P('row', 'col')
Inputs may be any that keep to these rules, and one draw needn't show every extreme that they name: `diag_blocks`: every block is symmetric and its eigenvalues are at least 1.
All inputs are finite; a program needn't handle non-finite values.
Results may differ from a plain program's by a relative error of at most 0.0054.
Values may be sent and summed in bfloat16 or wider, within the bound.
No kernel may reach another device: no remote copies, remote signals or barrier semaphores. Data moves between devices by JAX's collectives and lax.ppermute only.
A program may use at most 128 MiB of HBM per device.

v0:
```python
import jax
import jax.numpy as jnp
from jax import lax
from jax.sharding import PartitionSpec as P


def passed_along(value, axis, by):
    size = lax.axis_size(axis)
    return lax.ppermute(value, axis, [(i, (i + by) % size) for i in range(size)])


def select_colour(blocks, parity):
    grid_rows = blocks.shape[0]
    grid_columns = blocks.shape[1]
    trailing = blocks.shape[2:]
    paired = blocks.reshape((grid_rows // 2, 2, grid_columns // 2, 2) + trailing)
    joined = jnp.stack([paired[:, 0, :, parity], paired[:, 1, :, 1 - parity]], 1)
    return joined.reshape((grid_rows, grid_columns // 2) + trailing)


def combine_rows(even_rows, odd_rows):
    joined = jnp.stack([even_rows, odd_rows], 1)
    return joined.reshape((2 * even_rows.shape[0],) + even_rows.shape[1:])


def transposed(blocks):
    return jnp.swapaxes(blocks, -1, -2)


def gram_term(former, latter):
    return jnp.einsum("rmka,rmkb->rmab", former, latter, preferred_element_type=jnp.float32)


def on_device(diag_blocks, horizontal, vertical):
    edge_column = passed_along(horizontal[:, -1:], "col", 1)
    left_links = jnp.concatenate([edge_column, horizontal[:, :-1]], 1)
    edge_row = passed_along(vertical[-1:], "row", 1)
    upper_links = jnp.concatenate([edge_row, vertical[:-1]], 0)
    couplings = (
        transposed(select_colour(left_links, 0)).astype(jnp.float32),
        transposed(select_colour(upper_links, 0)).astype(jnp.float32),
        select_colour(horizontal, 0).astype(jnp.float32),
        select_colour(vertical, 0).astype(jnp.float32),
    )
    red_factor = jnp.linalg.cholesky(select_colour(diag_blocks, 0))
    results = [
        jax.scipy.linalg.solve_triangular(red_factor, coupling, lower=True)
        for coupling in couplings
    ]
    solved = jnp.stack(results, 2).astype(jnp.bfloat16)
    got_above = passed_along(solved[-1:, :, 3], "row", 1)
    above_down = jnp.concatenate([got_above, solved[:-1, :, 3]], 0)
    got_below = passed_along(solved[:1], "row", -1)
    below_all = jnp.concatenate([solved[1:], got_below], 0)
    got_left = passed_along(solved[1::2, -1:, 2:4], "col", 1)
    left_pair = combine_rows(
        solved[0::2, :, 2:4], jnp.concatenate([got_left, solved[1::2, :-1, 2:4]], 1)
    )
    right_first, right_rest = passed_along((solved[0::2, :1, 0], solved[0::2, :1, 2:4]), "col", -1)
    right_left = combine_rows(
        jnp.concatenate([solved[0::2, 1:, 0], right_first], 1), solved[1::2, :, 0]
    )
    right_pair = combine_rows(
        jnp.concatenate([solved[0::2, 1:, 2:4], right_rest], 1), solved[1::2, :, 2:4]
    )
    below_up = below_all[:, :, 1]
    update = gram_term(above_down, above_down) + gram_term(below_up, below_up)
    update = (
        update
        + gram_term(left_pair[:, :, 0], left_pair[:, :, 0])
        + gram_term(right_left, right_left)
    )
    black_schur = select_colour(diag_blocks, 1) - update
    east_link = -gram_term(right_left, right_pair[:, :, 0])
    south_link = -gram_term(below_up, below_all[:, :, 3])
    southeast = -(
        gram_term(right_left, right_pair[:, :, 1]) + gram_term(below_up, below_all[:, :, 2])
    )
    southwest = -(
        gram_term(left_pair[:, :, 0], left_pair[:, :, 1]) + gram_term(below_up, below_all[:, :, 0])
    )
    black_links = jnp.stack([east_link, south_link, southeast, southwest], 2).astype(jnp.bfloat16)
    return (red_factor, black_schur, black_links)


def solution(mesh):
    in_specs = (
        P("row", "col", None, None),
        P("row", "col", None, None),
        P("row", "col", None, None),
    )
    out_specs = (
        P("row", "col", None, None),
        P("row", "col", None, None),
        P("row", "col", None, None, None),
    )
    return jax.shard_map(
        on_device, mesh=mesh, in_specs=in_specs, out_specs=out_specs, check_vma=False
    )
```

profile of v0, /device:TPU:27, one launch (start us, length us, event | category | flops | bytes accessed | tf_op | source)
XLA Modules:
  0.0 403.3 jit_solution(7077710784273775207)
XLA Ops:
  0.6 2.7 fusion.145
  3.4 1.3 copy.153
  4.7 1.8 collective-permute-start.1
  6.6 5.2 %copy.62 = f32[2,2,512,512]{2,3,1,0:T(8,128)} copy(f32[2,2,512,512]{3,2,1,0:T(8,128)} %param.5) | data formatting | bytes 8388608 | tf_op args[0]
  11.8 4.2 %slice_bitcast_fusion.10 = (f32[1,1,1,512,512]{3,4,2,1,0:T(8,128)}, f32[1,1,1,512,512]{3,4,2,1,0:T(8,128)}, f32[1,1,1,512,512]{3,4,1,2,0:T(8,128)S(1)}, f32[1,1,1,512,512]{3,4,1,2,0:T(8,128)S(1)}) fusion(f32[1,2,1,2,512,512]{4,5,3,2,1,0:T(8,128)} %bitcast.342), kind=kLoop, calls=%fused_computation.110 | loop fusion | bytes 8388608 | tf_op jit(solution)/shard_map/stack;squeeze | solution.py:17
  16.0 1.5 fusion.7
  17.5 2.9 copy.64
  20.3 2.1 fusion.6
  22.4 1.3 copy-done.9
  23.8 23.5 %custom-call.34 = f32[2,1,128,128]{3,2,1,0:T(8,128)S(1)} custom-call(f32[2,1,128,128]{3,2,1,0:T(8,128)S(1)} %cholesky.283), custom_call_target="Cholesky" | custom-call | tf_op jit(solution)/shard_map/jit(cholesky)/cholesky | solution.py:45
  47.3 19.7 %custom-call.35 = f32[2,1,1,128,128]{3,4,2,1,0:T(8,128)S(1)} custom-call(f32[2,1,1,128,128]{4,3,2,1,0:T(8,128)S(1)} %select_bitcast_fusion.2), custom_call_target="InvertDiagBlocksLowerTriangular" | custom-call | tf_op jit(solution)/shard_map/jit(cholesky)/cholesky | solution.py:45
  67.2 1.5 constant_dynamic-update-slice_fusion.3
  68.7 1.5 fusion.47
  70.2 23.7 %custom-call.36 = f32[2,1,128,128]{3,2,1,0:T(8,128)S(1)} custom-call(f32[2,1,128,128]{3,2,1,0:T(8,128)S(1)} %cholesky.287), custom_call_target="Cholesky" | custom-call | tf_op jit(solution)/shard_map/jit(cholesky)/cholesky | solution.py:45
  93.9 19.7 %custom-call.37 = f32[2,1,1,128,128]{3,4,2,1,0:T(8,128)S(1)} custom-call(f32[2,1,1,128,128]{4,3,2,1,0:T(8,128)S(1)} %get-tuple-element.83), custom_call_target="InvertDiagBlocksLowerTriangular" | custom-call | tf_op jit(solution)/shard_map/jit(cholesky)/cholesky | solution.py:45
  114.0 1.6 fusion.49
  115.6 23.5 %custom-call.38 = f32[2,1,128,128]{3,2,1,0:T(8,128)S(1)} custom-call(f32[2,1,128,128]{3,2,1,0:T(8,128)S(1)} %cholesky.292), custom_call_target="Cholesky" | custom-call | tf_op jit(solution)/shard_map/jit(cholesky)/cholesky | solution.py:45
  139.1 20.1 %custom-call.39 = f32[2,1,1,128,128]{3,4,2,1,0:T(8,128)S(1)} custom-call(f32[2,1,1,128,128]{4,3,2,1,0:T(8,128)S(1)} %get-tuple-element.81), custom_call_target="InvertDiagBlocksLowerTriangular" | custom-call | tf_op jit(solution)/shard_map/jit(cholesky)/cholesky | solution.py:45
  159.4 1.5 fusion.51
  161.0 23.5 %custom-call.40 = f32[2,1,128,128]{3,2,1,0:T(8,128)S(1)} custom-call(f32[2,1,128,128]{3,2,1,0:T(8,128)S(1)} %fusion.51), custom_call_target="Cholesky" | custom-call | tf_op jit(solution)/shard_map/jit(cholesky)/cholesky | solution.py:45
  185.8 3.6 bitcast_select_fusion
  189.4 10.7 %while.8 = (s32[]{:T(128)}, f32[2,512,512]{2,1,0:T(8,128)S(1)}, s32[4,2]{0,1:T(2,128)S(1)}, f32[4,2,128,128]{3,2,0,1:T(8,128)}, s32[]{:T(128)}) while((s32[]{:T(128)}, f32[2,512,512]{2,1,0:T(8,128)S(1)}, s32[4,2]{0,1:T(2,128)S(1)}, f32[4,2,128,128]{3,2,0,1:T(8,128)}, s32[]{:T(128)}) %tuple.60), condition=%wide.while_cond, body=%wide.while_body.sunk | while | flops 2 | bytes 263777 | solution.py:47
  190.1 2.1 bitcast_dynamic-update-slice_fusion.2
  192.7 2.0 bitcast_dynamic-update-slice_fusion.2
  195.4 2.0 bitcast_dynamic-update-slice_fusion.2
  198.1 2.1 bitcast_dynamic-update-slice_fusion.2
  200.1 79.6 %custom-call.44 = f32[2,4,128,128]{2,3,1,0:T(8,128)S(1)} custom-call(f32[2,4,128,128]{3,2,1,0:T(8,128)} %bitcast.350), custom_call_target="InvertDiagBlocksLowerTriangular" | custom-call | tf_op jit(solution)/shard_map/jit(_solve_triangular)/vmap()/triangular_solve | solution.py:47
  279.7 1.5 slice_bitcast_fusion.17
  284.6 1.1 fusion.35
  287.8 1.6 fusion.113
  292.9 2.3 fusion.142
  295.4 1.6 fusion.146
  297.0 2.3 copy.155
  299.3 1.2 fusion.2
  301.5 1.3 collective-permute-start
  302.8 1.5 copy.154
  304.3 1.5 copy.156
  305.8 1.7 maximum_bitcast_fusion.2
  311.9 1.1 fusion.41
  313.8 9.9 %collective-permute-done.2 = bf16[1,2,512,512]{2,3,1,0:T(8,128)(2,1)} collective-permute-done((bf16[1,2,512,512]{2,3,1,0:T(8,128)(2,1)}, bf16[1,2,512,512]{2,3,1,0:T(8,128)(2,1)}, u32[]{:S(2)}, u32[]{:S(2)}) %collective-permute-start.2) | collective-permute-done | bytes 1048608 | tf_op jit(solution)/shard_map/ppermute | solution.py:9
  323.7 1.4 maximum_bitcast_fusion.4
  333.0 4.9 %collective-permute-start.4 = (bf16[1,1,2,512,512]{4,3,2,1,0:T(8,128)(2,1)S(1)}, bf16[1,1,2,512,512]{4,3,2,1,0:T(8,128)(2,1)S(1)}, u32[]{:S(2)}, u32[]{:S(2)}) collective-permute-start(bf16[1,1,2,512,512]{4,3,2,1,0:T(8,128)(2,1)S(1)} %copy-done.16), channel_id=1, source_target_pairs={{0,1},{1,2},{2,3},{3,4},{4,5},{5,6},{6,7},{7,0},{8,9},{9,10},{10,1... | collective-permute-start | bytes 3145736 | tf_op jit(solution)/shard_map/ppermute | solution.py:9
  337.9 1.9 fusion.74
  341.2 1.5 maximum_bitcast_fusion.8
  342.7 12.5 %collective-permute-done.4 = bf16[1,1,2,512,512]{4,3,2,1,0:T(8,128)(2,1)S(1)} collective-permute-done((bf16[1,1,2,512,512]{4,3,2,1,0:T(8,128)(2,1)S(1)}, bf16[1,1,2,512,512]{4,3,2,1,0:T(8,128)(2,1)S(1)}, u32[]{:S(2)}, u32[]{:S(2)}) %collective-permute-start.4) | collective-permute-done | bytes 1048608 | tf_op jit(solution)/shard_map/ppermute | solution.py:9
  356.3 35.2 %collective-permute-done.5 = bf16[1,1,512,512]{3,2,1,0:T(8,128)(2,1)S(1)} collective-permute-done((bf16[1,1,512,512]{3,2,1,0:T(8,128)(2,1)S(1)}, bf16[1,1,512,512]{3,2,1,0:T(8,128)(2,1)S(1)}, u32[]{:S(2)}, u32[]{:S(2)}) %collective-permute-start.5) | collective-permute-done | bytes 524320 | tf_op jit(solution)/shard_map/ppermute | solution.py:9
  397.6 2.5 copy.117
  401.0 1.8 copy.116
  (125 shorter events, 37.0 us)
Async XLA Ops:
  4.7 301.1 %collective-permute-start.1 = (bf16[2,1,512,512]{2,3,1,0:T(8,128)(2,1)}, bf16[2,1,512,512]{2,3,1,0:T(8,128)(2,1)}, u32[]{:S(2)}, u32[]{:S(2)}) collective-permute-start(bf16[2,1,512,512]{2,3,1,0:T(8,128)(2,1)} %copy.153), channel_id=1, source_target_pairs={{0,1},{1,2},{2,3},{3,4},{4,5},{5,6},{6,7},{7,0},{8,9},{9,10},{10,1... | collective-permute-start | bytes 3145736 | tf_op jit(solution)/shard_map/ppermute | solution.py:9
  22.4 1.3 copy-start.9
  184.5 1.3 copy-start
  279.7 6.9 %copy-start.5 = (f32[2,4,128,128]{2,3,1,0:T(8,128)}, f32[2,4,128,128]{2,3,1,0:T(8,128)S(1)}, u32[]{:S(2)}) copy-start(f32[2,4,128,128]{2,3,1,0:T(8,128)S(1)} %custom-call.44) | copy-start | bytes 1572868
  284.6 1.8 copy-start.10
  287.8 2.3 copy-start.6
  290.8 1.9 copy-start.8
  292.7 2.4 copy-start.1
  292.9 2.5 copy-start.3
  295.4 44.8 %collective-permute-start.6 = (bf16[1,1,2,512,512]{4,3,2,1,0:T(8,128)(2,1)}, bf16[1,1,2,512,512]{4,3,2,1,0:T(8,128)(2,1)}, u32[]{:S(2)}, u32[]{:S(2)}) collective-permute-start(bf16[1,1,2,512,512]{4,3,2,1,0:T(8,128)(2,1)} %get-tuple-element.62), channel_id=1, source_target_pairs={{0,7},{1,0},{2,1},{3,2},{4,3},{5,4},{6,5},{7,6},{8,15},{9,8},{10,9... | collective-permute-start | bytes 3145736 | tf_op jit(solution)/shard_map/ppermute | solution.py:9
  299.3 24.4 %collective-permute-start.2 = (bf16[1,2,512,512]{2,3,1,0:T(8,128)(2,1)}, bf16[1,2,512,512]{2,3,1,0:T(8,128)(2,1)}, u32[]{:S(2)}, u32[]{:S(2)}) collective-permute-start(bf16[1,2,512,512]{2,3,1,0:T(8,128)(2,1)} %copy.155), channel_id=1, source_target_pairs={{0,8},{8,16},{16,24},{24,0},{1,9},{9,17},{17,25},{25,1},{2,10},{10... | collective-permute-start | bytes 3145736 | tf_op jit(solution)/shard_map/ppermute | solution.py:9
  300.5 2.3 copy-start.11
  301.5 36.4 %collective-permute-start = (bf16[1,1,512,512]{3,2,0,1:T(8,128)(2,1)}, bf16[1,1,512,512]{3,2,0,1:T(8,128)(2,1)}, u32[]{:S(2)}, u32[]{:S(2)}) collective-permute-start(bf16[1,1,512,512]{3,2,0,1:T(8,128)(2,1)} %get-tuple-element.78), channel_id=1, source_target_pairs={{0,8},{8,16},{16,24},{24,0},{1,9},{9,17},{17,25},{25,1},{2,10},{10... | collective-permute-start | bytes 1572872 | tf_op jit(solution)/shard_map/ppermute | solution.py:9
  307.6 1.0 copy-start.7
  329.7 1.2 copy-start.2
  329.7 1.5 copy-start.4
  331.8 1.2 copy-start.16
  331.8 6.1 %copy-start.17 = (bf16[1,1,512,512]{3,2,0,1:T(8,128)(2,1)S(1)}, bf16[1,1,512,512]{3,2,0,1:T(8,128)(2,1)}, u32[]{:S(2)}) copy-start(bf16[1,1,512,512]{3,2,0,1:T(8,128)(2,1)} %get-tuple-element.79) | copy-start | bytes 1572868
  332.1 60.2 %collective-permute-start.3 = (bf16[1,1,4,512,512]{4,3,0,2,1:T(8,128)(2,1)S(1)}, bf16[1,1,4,512,512]{4,3,0,2,1:T(8,128)(2,1)S(1)}, u32[]{:S(2)}, u32[]{:S(2)}) collective-permute-start(bf16[1,1,4,512,512]{4,3,0,2,1:T(8,128)(2,1)S(1)} %get-tuple-element.56), channel_id=1, source_target_pairs={{0,24},{8,0},{16,8},{24,16},{1,25},{9,1},{17,9},{25,17},{2,26},{10... | collective-permute-start | bytes 6291464 | tf_op jit(solution)/shard_map/ppermute | solution.py:9
  333.0 22.3 %collective-permute-start.4 = (bf16[1,1,2,512,512]{4,3,2,1,0:T(8,128)(2,1)S(1)}, bf16[1,1,2,512,512]{4,3,2,1,0:T(8,128)(2,1)S(1)}, u32[]{:S(2)}, u32[]{:S(2)}) collective-permute-start(bf16[1,1,2,512,512]{4,3,2,1,0:T(8,128)(2,1)S(1)} %copy-done.16), channel_id=1, source_target_pairs={{0,1},{1,2},{2,3},{3,4},{4,5},{5,6},{6,7},{7,0},{8,9},{9,10},{10,1... | collective-permute-start | bytes 3145736 | tf_op jit(solution)/shard_map/ppermute | solution.py:9
  340.0 1.2 copy-start.13
  340.0 51.5 %collective-permute-start.5 = (bf16[1,1,512,512]{3,2,1,0:T(8,128)(2,1)S(1)}, bf16[1,1,512,512]{3,2,1,0:T(8,128)(2,1)S(1)}, u32[]{:S(2)}, u32[]{:S(2)}) collective-permute-start(bf16[1,1,512,512]{3,2,1,0:T(8,128)(2,1)S(1)} %slice.292), channel_id=1, source_target_pairs={{0,7},{1,0},{2,1},{3,2},{4,3},{5,4},{6,5},{7,6},{8,15},{9,8},{10,9... | collective-permute-start | bytes 1572872 | tf_op jit(solution)/shard_map/ppermute | solution.py:9
  341.2 14.0 %copy-start.12 = (bf16[1,1,1,2,512,512]{5,4,3,2,1,0:T(8,128)(2,1)S(1)}, bf16[1,1,1,2,512,512]{5,4,3,2,1,0:T(8,128)(2,1)}, u32[]{:S(2)}) copy-start(bf16[1,1,1,2,512,512]{5,4,3,2,1,0:T(8,128)(2,1)} %get-tuple-element.63) | copy-start | bytes 3145732
  397.6 2.5 copy-start.14
  397.6 2.5 copy-start.15
where the time goes:
time: 411 us; the launch traced here: 403 us
  other arithmetic  252 us (61%)
  waiting for transfers between devices  57.7 us (14%)
  local copies, waits for them, and re-layouts  47.4 us (12%)
  matrix products  36.4 us (9%)
  starting transfers between devices  8.25 us (2%)
    another operation x16, other arithmetic, on_device(): red_factor = jnp.linalg.cholesky(select_colour(diag_blocks, 0))  154 us
    another operation x4, other arithmetic, on_device(): jax.scipy.linalg.solve_triangular(red_factor, coupling, lower=True)  83.2 us
    ppermute x7, waiting for transfers between devices, passed_along(): lax.ppermute(value, axis, [(i, (i + by) % size) for i in range(size)])  57.7 us
    unnamed x43, local copies, waits for them, and re-layouts  22 us
    another operation x28, matrix products, on_device(): jax.scipy.linalg.solve_triangular(red_factor, coupling, lower=True)  20.7 us
    another operation x13, local copies, waits for them, and re-layouts, on_device(): jax.scipy.linalg.solve_triangular(red_factor, coupling, lower=True)  10.7 us
    dot_general x10, matrix products, gram_term(): jnp.einsum('rmka,rmkb->rmab', former, latter, preferred_element_type=jnp....  8.94 us
    ppermute x7, starting transfers between devices, passed_along(): lax.ppermute(value, axis, [(i, (i + by) % size) for i in range(size)])  8.25 us
  transfers between devices with their start and end apart: 7, of which 3 were waited for; matrix products, arithmetic and copies ran while one was open for 78% of the time, Pallas kernels for 0%

commit v1 on v0

--- a/solution.py
+++ b/solution.py
@@ -1,7 +1,159 @@
 import jax
 import jax.numpy as jnp
 from jax import lax
+from jax.experimental import pallas as pl
+from jax.experimental.pallas import tpu as pltpu
 from jax.sharding import PartitionSpec as P
+
+F32 = jnp.float32
+BF16 = jnp.bfloat16
+LANES = 128
+SUB = 8
+STEP = 16
+
+
+def split(value):
+    high = value.astype(BF16)
+    low = (value - high.astype(F32)).astype(BF16)
+    return high, low
+
+
+def dot3(left, right, left_dim):
+    lh, ll = split(left)
+    rh, rl = split(right)
+    lefts = jnp.concatenate([lh, lh, ll], left_dim)
+    rights = jnp.concatenate([rh, rl, rh], 0)
+    return lax.dot_general(lefts, rights, (((left_dim,), (0,)), ((), ())), preferred_element_type=F32)
+
+
+def spread_row(tile, i):
+    return jnp.broadcast_to(tile[i : i + 1, :], (SUB, LANES))
+
+
+def eliminate(rows, first, below):
+    tiles = len(rows)
+    cols = [
+        [jnp.broadcast_to(rows[t][0][:, first + m : first + m + 1], (SUB, LANES)) for t in range(tiles)]
+        for m in range(STEP)
+    ]
+    roots = [None] * STEP
+    for i in range(STEP):
+        t0, s = divmod(i, SUB)
+        pivot = spread_row(cols[i][t0], s)
+        inverse = 1.0 / pivot
+        roots[i] = pivot
+        factor = [None] * tiles
+        for t in range(t0, tiles):
+            factor[t] = cols[i][t] * inverse
+        factor[t0] = jnp.where(below[s], factor[t0], 0.0)
+        for m in range(i + 1, STEP):
+            top = spread_row(cols[m][t0], s)
+            for t in range(t0, tiles):
+                cols[m][t] = cols[m][t] - factor[t] * top
+        for g in range(len(rows[0])):
+            top = spread_row(rows[t0][g], s)
+            for t in range(t0, tiles):
+                rows[t][g] = rows[t][g] - factor[t] * top
+    scales = []
+    sub = lax.broadcasted_iota(jnp.int32, (SUB, LANES), 0)
+    for t in range(STEP // SUB):
+        piv = roots[t * SUB]
+        for s in range(1, SUB):
+            piv = jnp.where(sub == s, roots[t * SUB + s], piv)
+        scales.append(lax.rsqrt(piv))
+    return scales
+
+
+def factor_body(diags, factors, highs, lows, works, exts, tiles):
+    size = works[0].shape[0]
+    count = size // LANES
+    sub = lax.broadcasted_iota(jnp.int32, (SUB, LANES), 0)
+    below = [sub > s for s in range(SUB)]
+    r = lax.broadcasted_iota(jnp.int32, (LANES, LANES), 0)
+    c = lax.broadcasted_iota(jnp.int32, (LANES, LANES), 1)
+    eye = jnp.where(r == c, 1.0, 0.0).astype(F32)
+    n = len(works)
+    for x in range(n):
+        works[x][...] = diags[x][...]
+        exts[x][...] = jnp.zeros(exts[x].shape, F32)
+    for k in range(count):
+        lo, hi = k * LANES, (k + 1) * LANES
+        for x in range(n):
+            tiles[x][:, :LANES] = works[x][lo:hi, lo:hi]
+            tiles[x][:, LANES:] = eye
+        for p in range(LANES // STEP):
+            for x in range(n):
+                start = p * STEP
+                stop = min(start + 2 * STEP, LANES)
+                rows = [
+                    [tiles[x][start + SUB * t : start + SUB * (t + 1), g * LANES : (g + 1) * LANES] for g in range(2)]
+                    for t in range((stop - start) // SUB)
+                ]
+                scales = eliminate(rows, start, below)
+                for t in range(len(rows)):
+                    for g in range(2):
+                        v = rows[t][g]
+                        if t < STEP // SUB:
+                            v = v * scales[t]
+                            rows[t][g] = v
+                        tiles[x][start + SUB * t : start + SUB * (t + 1), g * LANES : (g + 1) * LANES] = v
+                if stop < LANES:
+                    done = jnp.concatenate([jnp.concatenate(rows[t], 1) for t in range(STEP // SUB)], 0)
+                    update = dot3(done[:, :LANES], done, 0)
+                    tiles[x][stop:, :] = tiles[x][stop:, :] - update[stop:, :]
+        for x in range(n):
+            upper = jnp.where(c >= r, tiles[x][:, :LANES], 0.0)
+            inv = jnp.where(c <= r, tiles[x][:, LANES:], 0.0)
+            works[x][lo:hi, lo:hi] = upper
+            exts[x][lo:hi, lo:hi] = inv
+            if k:
+                exts[x][lo:hi, :lo] = dot3(inv, exts[x][lo:hi, :lo], 1)
+            if hi < size:
+                works[x][lo:hi, hi:] = dot3(inv, works[x][lo:hi, hi:], 1)
+                panel = works[x][lo:hi, hi:]
+                works[x][hi:, hi:] = works[x][hi:, hi:] - dot3(panel, panel, 0)
+                exts[x][hi:, :hi] = exts[x][hi:, :hi] - dot3(panel, exts[x][lo:hi, :hi], 0)
+    for x in range(n):
+        for k in range(count):
+            lo, hi = k * LANES, (k + 1) * LANES
+            for q in range(count):
+                a, b = q * LANES, (q + 1) * LANES
+                if q <= k:
+                    factors[x][lo:hi, a:b] = works[x][a:b, lo:hi].T
+                else:
+                    factors[x][lo:hi, a:b] = jnp.zeros((LANES, LANES), F32)
+        w = exts[x][...]
+        h, l = split(w)
+        highs[x][...] = h
+        lows[x][...] = l
+
+
+def factor_kernel(first, second, factor, high, low, w0, w1, e0, e1, t0, t1):
+    factor_body(
+        [first.at[0, 0], second.at[0, 0]],
+        [factor.at[0, 0], factor.at[1, 0]],
+        [high.at[0, 0], high.at[1, 0]],
+        [low.at[0, 0], low.at[1, 0]],
+        [w0, w1], [e0, e1], [t0, t1],
+    )
+
+
+def factorize(diag_blocks):
+    rows, columns, size, _ = diag_blocks.shape
+    shape = (rows, columns // 2, size, size)
+    out_spec = pl.BlockSpec((2, 1, size, size), lambda a, m: (a, m, 0, 0))
+    return pl.pallas_call(
+        factor_kernel,
+        grid=(rows // 2, columns // 2),
+        in_specs=[
+            pl.BlockSpec((1, 1, size, size), lambda a, m: (2 * a, 2 * m, 0, 0)),
+            pl.BlockSpec((1, 1, size, size), lambda a, m: (2 * a + 1, 2 * m + 1, 0, 0)),
+        ],
+        out_specs=[out_spec, out_spec, out_spec],
+        out_shape=[jax.ShapeDtypeStruct(shape, F32), jax.ShapeDtypeStruct(shape, BF16), jax.ShapeDtypeStruct(shape, BF16)],
+        scratch_shapes=[pltpu.VMEM((size, size), F32)] * 4 + [pltpu.VMEM((LANES, 2 * LANES), F32)] * 2,
+        name="factor",
+    )(diag_blocks, diag_blocks)
 
 
 def passed_along(value, axis, by):
@@ -31,22 +183,23 @@
     return jnp.einsum("rmka,rmkb->rmab", former, latter, preferred_element_type=jnp.float32)
 
 
+def apply_inverse(inverse, coupling):
+    return jnp.einsum("rmak,rmkb->rmab", inverse, coupling, preferred_element_type=jnp.float32)
+
+
 def on_device(diag_blocks, horizontal, vertical):
     edge_column = passed_along(horizontal[:, -1:], "col", 1)
     left_links = jnp.concatenate([edge_column, horizontal[:, :-1]], 1)
     edge_row = passed_along(vertical[-1:], "row", 1)
     upper_links = jnp.concatenate([edge_row, vertical[:-1]], 0)
     couplings = (
-        transposed(select_colour(left_links, 0)).astype(jnp.float32),
-        transposed(select_colour(upper_links, 0)).astype(jnp.float32),
-        select_colour(horizontal, 0).astype(jnp.float32),
-        select_colour(vertical, 0).astype(jnp.float32),
-    )
-    red_factor = jnp.linalg.cholesky(select_colour(diag_blocks, 0))
-    results = [
-        jax.scipy.linalg.solve_triangular(red_factor, coupling, lower=True)
-        for coupling in couplings
-    ]
+        transposed(select_colour(left_links, 0)),
+        transposed(select_colour(upper_links, 0)),
+        select_colour(horizontal, 0),
+        select_colour(vertical, 0),
+    )
+    red_factor, high, low = factorize(diag_blocks)
+    results = [apply_inverse(high, coupling) + apply_inverse(low, coupling) for coupling in couplings]
     solved = jnp.stack(results, 2).astype(jnp.bfloat16)
     got_above = passed_along(solved[-1:, :, 3], "row", 1)
     above_down = jnp.concatenate([got_above, solved[:-1, :, 3]], 0)

time: 411 us -> 126 us (0.31); the launches traced: 403 us -> 124 us
  other arithmetic: 252 us -> 4.74 us
  local copies, waits for them, and re-layouts: 47.4 us -> 10.7 us
  Pallas kernels: 0 us -> 23.3 us
  matrix products: 36.4 us -> 15 us
    another operation x24 -> x1, other arithmetic: 239 us -> 0.1 us  [the longest x16 154 us: on_device(): red_factor = jnp.linalg.cholesky(select_colour(diag_blocks, 0))]
    another operation x34 -> x0, matrix products: 27.5 us -> none  [the longest x28 20.7 us: on_device(): jax.scipy.linalg.solve_triangular(red_factor, coupling, lower=True)]
    pallas_call x0 -> x1, Pallas kernels: none -> 23.3 us  [factorize(): pl.pallas_call(factor_kernel, grid=(rows // 2, columns // 2), in_specs=[p...]
    unnamed x43 -> x13, local copies, waits for them, and re-layouts: 22 us -> 5.47 us
    another operation x17 -> x0, local copies, waits for them, and re-layouts: 11 us -> none  [the longest x13 10.7 us: on_device(): jax.scipy.linalg.solve_triangular(red_factor, coupling, lower=True)]
    dot_general x0 -> x8, matrix products: none -> 5.87 us  [apply_inverse(): jnp.einsum('rmak,rmkb->rmab', inverse, coupling, preferred_element_type=j...]
    another operation x5, local copies, waits for them, and re-layouts: 5.82 us -> 0.45 us  [select_colour(): jnp.stack([paired[:, 0, :, parity], paired[:, 1, :, 1 - parity]], 1)]
  transfers between devices with their start and end apart: 7 -> 7, of which waited for: 3 -> 2; matrix products, arithmetic and copies ran while one was open for 78% -> 8% of each run, Pallas kernels for 0% -> 19%
where the time goes in v1:
time: 126 us; the launch traced here: 124 us
  waiting for transfers between devices  61 us (48%)
  Pallas kernels  23.3 us (18%)
  matrix products  15 us (12%)
  local copies, waits for them, and re-layouts  10.7 us (8%)
  starting transfers between devices  8.87 us (7%)
  other arithmetic  4.74 us (4%)
    ppermute x7, waiting for transfers between devices, passed_along(): lax.ppermute(value, axis, [(i, (i + by) % size) for i in range(size)])  61 us
    pallas_call x1, Pallas kernels, factorize(): pl.pallas_call(factor_kernel, grid=(rows // 2, columns // 2), in_specs=[p...  23.3 us
    dot_general x10, matrix products, gram_term(): jnp.einsum('rmka,rmkb->rmab', former, latter, preferred_element_type=jnp....  9.09 us
    ppermute x7, starting transfers between devices, passed_along(): lax.ppermute(value, axis, [(i, (i + by) % size) for i in range(size)])  8.87 us
    dot_general x8, matrix products, apply_inverse(): jnp.einsum('rmak,rmkb->rmab', inverse, coupling, preferred_element_type=j...  5.87 us
    unnamed x13, local copies, waits for them, and re-layouts  5.47 us
    slice x1, local copies, waits for them, and re-layouts, on_device(): edge_column = passed_along(horizontal[:, -1:], 'col', 1)  3.14 us
    reshape x2, other arithmetic, select_colour(): blocks.reshape((grid_rows // 2, 2, grid_columns // 2, 2) + trailing)  2.84 us
  transfers between devices with their start and end apart: 7, of which 2 were waited for; matrix products, arithmetic and copies ran while one was open for 8% of the time, Pallas kernels for 19%

profile of v1, /device:TPU:27, one launch (start us, length us, event | category | flops | bytes accessed | tf_op | source)
XLA Modules:
  0.0 124.5 jit_solution(4886535943333664293)
XLA Ops:
  0.6 3.1 %fusion.59 = (bf16[2,1,512,512]{3,2,1,0:T(8,128)(2,1)}, bf16[2,1,512,512]{3,2,1,0:T(8,128)(2,1)}) fusion(bf16[2,2,512,512]{3,2,1,0:T(8,128)(2,1)} %param.4), kind=kLoop, calls=%fused_computation.105 | loop fusion | bytes 4194304 | tf_op jit(solution)/shard_map/slice | solution.py:191
  3.8 1.8 %collective-permute-start.1 = (bf16[2,1,512,512]{3,2,1,0:T(8,128)(2,1)}, bf16[2,1,512,512]{3,2,1,0:T(8,128)(2,1)}, u32[]{:S(2)}, u32[]{:S(2)}) collective-permute-start(bf16[2,1,512,512]{3,2,1,0:T(8,128)(2,1)} %get-tuple-element.22), channel_id=1, source_target_pairs={{0,1},{1,2},{2,3},{3,4},{4,5},{5,6},{6,7},{7,0},{8,9},{9,10},{10,1... | collective-permute-start | bytes 3145736 | tf_op jit(solution)/shard_map/ppermute | solution.py:161
  5.6 1.2 fusion.60
  6.7 23.3 %factor.1 = (f32[2,1,512,512]{3,2,1,0:T(8,128)}, bf16[2,1,512,512]{3,2,1,0:T(8,128)(2,1)}, bf16[2,1,512,512]{3,2,1,0:T(8,128)(2,1)}) custom-call(f32[2,2,512,512]{3,2,1,0:T(8,128)} %second.1, f32[2,2,512,512]{3,2,1,0:T(8,128)} %second.1), custom_call_target="tpu_custom_call" | custom-call | tf_op jit(solution)/shard_map/factor/pallas_call | solution.py:145
  30.2 1.2 copy-done.2
  31.3 0.7 fusion.36
  32.0 0.9 copy-done.4
  33.0 0.7 fusion.30
  33.7 0.5 copy-done.1
  34.2 0.7 fusion.3
  34.9 0.7 add_convert_fusion.3
  35.7 0.5 copy-done.5
  36.2 1.4 %maximum_bitcast_fusion.1 = bf16[1,2,1,2,512,512]{5,4,3,2,1,0:T(8,128)(2,1)S(1)} fusion(bf16[2,1,512,512]{3,2,1,0:T(8,128)(2,1)S(1)} %copy-done.5, bf16[2,1,512,512]{3,2,1,0:T(8,128)(2,1)} %collective-permute-done.1), kind=kLoop, calls=%fused_computation.11 | loop fusion | flops 1048576 | bytes 4194304 | tf_op jit(solution)/shard_map/reshape | solution.py:168
  37.6 0.1 slice_bitcast_fusion.20
  37.6 0.7 fusion.34
  38.4 0.7 add_convert_fusion.2
  39.2 1.4 %maximum_bitcast_fusion.2 = bf16[1,2,1,2,512,512]{5,4,3,2,1,0:T(8,128)(2,1)S(1)} fusion(bf16[1,2,512,512]{3,2,1,0:T(8,128)(2,1)S(1)} %get-tuple-element.27, bf16[1,2,512,512]{3,2,1,0:T(8,128)(2,1)} %collective-permute-done.2), kind=kLoop, calls=%fused_computation.12 | loop fusion | flops 1048576 | bytes 4194304 | tf_op jit(solution)/shard_map/reshape | solution.py:168
  40.6 0.1 slice_bitcast_fusion.18
  40.7 0.8 fusion.32
  41.4 0.7 fusion.2
  42.2 0.6 pad_maximum_fusion
  42.8 0.3 fusion.58
  43.0 1.5 %collective-permute-start.3 = (bf16[1,1,4,512,512]{4,3,0,2,1:T(8,128)(2,1)S(1)}, bf16[1,1,4,512,512]{4,3,0,2,1:T(8,128)(2,1)S(1)}, u32[]{:S(2)}, u32[]{:S(2)}) collective-permute-start(bf16[1,1,4,512,512]{4,3,0,2,1:T(8,128)(2,1)S(1)} %get-tuple-element.12), channel_id=1, source_target_pairs={{0,24},{8,0},{16,8},{24,16},{1,25},{9,1},{17,9},{25,17},{2,26},{10... | collective-permute-start | bytes 6291464 | tf_op jit(solution)/shard_map/ppermute | solution.py:161
  44.5 0.3 fusion.57
  44.8 0.3 collective-permute-start.6
  45.1 0.1 slice_bitcast_fusion.22
  45.2 1.9 %collective-permute-start = (bf16[1,1,512,512]{3,2,1,0:T(8,128)(2,1)S(1)}, bf16[1,1,512,512]{3,2,1,0:T(8,128)(2,1)S(1)}, u32[]{:S(2)}, u32[]{:S(2)}) collective-permute-start(bf16[1,1,512,512]{3,2,1,0:T(8,128)(2,1)S(1)} %get-tuple-element.34), channel_id=1, source_target_pairs={{0,8},{8,16},{16,24},{24,0},{1,9},{9,17},{17,25},{25,1},{2,10},{10... | collective-permute-start | bytes 1572872 | tf_op jit(solution)/shard_map/ppermute | solution.py:161
  47.0 2.9 %collective-permute-start.4 = (bf16[1,1,2,512,512]{4,3,2,1,0:T(8,128)(2,1)S(1)}, bf16[1,1,2,512,512]{4,3,2,1,0:T(8,128)(2,1)S(1)}, u32[]{:S(2)}, u32[]{:S(2)}) collective-permute-start(bf16[1,1,2,512,512]{4,3,2,1,0:T(8,128)(2,1)S(1)} %get-tuple-element.18), channel_id=1, source_target_pairs={{0,1},{1,2},{2,3},{3,4},{4,5},{5,6},{6,7},{7,0},{8,9},{9,10},{10,1... | collective-permute-start | bytes 3145736 | tf_op jit(solution)/shard_map/ppermute | solution.py:161
  50.0 0.2 slice_bitcast_fusion.10
  50.1 53.1 %collective-permute-done = bf16[1,1,512,512]{3,2,1,0:T(8,128)(2,1)S(1)} collective-permute-done((bf16[1,1,512,512]{3,2,1,0:T(8,128)(2,1)S(1)}, bf16[1,1,512,512]{3,2,1,0:T(8,128)(2,1)S(1)}, u32[]{:S(2)}, u32[]{:S(2)}) %collective-permute-start) | collective-permute-done | bytes 524320 | tf_op jit(solution)/shard_map/ppermute | solution.py:161
  103.3 0.8 fusion.23
  104.0 0.1 slice_bitcast_fusion.14
  104.1 0.5 collective-permute-start.5
  104.7 0.2 maximum_bitcast_fusion.4
  104.9 0.2 maximum_bitcast_fusion.3
  105.1 0.8 fusion.38
  105.8 7.8 %collective-permute-done.5 = bf16[1,1,512,512]{3,2,1,0:T(8,128)(2,1)S(1)} collective-permute-done((bf16[1,1,512,512]{3,2,1,0:T(8,128)(2,1)S(1)}, bf16[1,1,512,512]{3,2,1,0:T(8,128)(2,1)S(1)}, u32[]{:S(2)}, u32[]{:S(2)}) %collective-permute-start.5) | collective-permute-done | bytes 524320 | tf_op jit(solution)/shard_map/ppermute | solution.py:161
  113.7 0.8 fusion.4
  114.5 0.1 fusion.14
  114.6 0.8 fusion.61
  115.3 0.8 fusion.11
  116.1 0.8 fusion.6
  116.9 0.8 fusion.19
  117.6 0.8 fusion.7
  118.4 0.8 fusion.5
  119.2 0.6 pad_maximum_fusion.1
  119.8 2.5 %copy.24 = bf16[2,1,4,512,512]{4,3,2,1,0:T(8,128)(2,1)} copy(bf16[2,1,4,512,512]{4,3,0,2,1:T(8,128)(2,1)S(1)} %pad_maximum_fusion.1) | data formatting | bytes 8388608
  122.3 2.2 %fusion.1 = f32[2,1,512,512]{3,2,1,0:T(8,128)} fusion(f32[1,1,1,512,512]{4,3,1,2,0:T(8,128)S(1)} %get-tuple-element.15, f32[1,1,1,512,512]{4,3,1,2,0:T(8,128)S(1)} %get-tuple-element.14, f32[2,512,512]{2,1,0:T(8,128)S(1)} %fusion.38, f32[2,512,512]{2,1,0:T(8,128)S(1)} %fusion.23, f32[2,512,512]{2,1,0:T(8,128)S(1)} %fusion.61, ...), kind=kOutput, calls=%fused_computation.10 | convolution fusion | flops 540016640 | bytes 11534336 | tf_op jit(solution)/shard_map/rmka,rmkb->rmab/dot_general | solution.py:183
  (16 shorter events, 0.2 us)
Async XLA Ops:
  0.6 4.9 %copy-start.3 = (bf16[2,2,512,512]{3,2,1,0:T(8,128)(2,1)S(1)}, bf16[2,2,512,512]{3,2,1,0:T(8,128)(2,1)}, u32[]{:S(2)}) copy-start(bf16[2,2,512,512]{3,2,1,0:T(8,128)(2,1)} %param.5) | copy-start | bytes 6291460
  3.8 31.9 %collective-permute-start.1 = (bf16[2,1,512,512]{3,2,1,0:T(8,128)(2,1)}, bf16[2,1,512,512]{3,2,1,0:T(8,128)(2,1)}, u32[]{:S(2)}, u32[]{:S(2)}) collective-permute-start(bf16[2,1,512,512]{3,2,1,0:T(8,128)(2,1)} %get-tuple-element.22), channel_id=1, source_target_pairs={{0,1},{1,2},{2,3},{3,4},{4,5},{5,6},{6,7},{7,0},{8,9},{9,10},{10,1... | collective-permute-start | bytes 3145736 | tf_op jit(solution)/shard_map/ppermute | solution.py:161
  6.7 32.4 %collective-permute-start.2 = (bf16[1,2,512,512]{3,2,1,0:T(8,128)(2,1)}, bf16[1,2,512,512]{3,2,1,0:T(8,128)(2,1)}, u32[]{:S(2)}, u32[]{:S(2)}) collective-permute-start(bf16[1,2,512,512]{3,2,1,0:T(8,128)(2,1)} %get-tuple-element.26), channel_id=1, source_target_pairs={{0,8},{8,16},{16,24},{24,0},{1,9},{9,17},{17,25},{25,1},{2,10},{10... | collective-permute-start | bytes 3145736 | tf_op jit(solution)/shard_map/ppermute | solution.py:161
  30.1 1.2 copy-start.2
  31.3 1.6 %copy-start.4 = (bf16[2,2,512,512]{3,2,1,0:T(8,128)(2,1)S(1)}, bf16[2,2,512,512]{3,2,1,0:T(8,128)(2,1)}, u32[]{:S(2)}) copy-start(bf16[2,2,512,512]{3,2,1,0:T(8,128)(2,1)} %param.4) | copy-start | bytes 6291460
  33.0 1.2 copy-start.1
  34.9 1.2 copy-start.5
  43.0 71.4 %collective-permute-start.3 = (bf16[1,1,4,512,512]{4,3,0,2,1:T(8,128)(2,1)S(1)}, bf16[1,1,4,512,512]{4,3,0,2,1:T(8,128)(2,1)S(1)}, u32[]{:S(2)}, u32[]{:S(2)}) collective-permute-start(bf16[1,1,4,512,512]{4,3,0,2,1:T(8,128)(2,1)S(1)} %get-tuple-element.12), channel_id=1, source_target_pairs={{0,24},{8,0},{16,8},{24,16},{1,25},{9,1},{17,9},{25,17},{2,26},{10... | collective-permute-start | bytes 6291464 | tf_op jit(solution)/shard_map/ppermute | solution.py:161
  44.5 5.4 %copy-start = (f32[2,2,512,512]{3,2,1,0:T(8,128)S(1)}, f32[2,2,512,512]{3,2,1,0:T(8,128)}, u32[]{:S(2)}) copy-start(f32[2,2,512,512]{3,2,1,0:T(8,128)} %second.1) | copy-start | bytes 12582916
  44.8 59.8 %collective-permute-start.6 = (bf16[1,1,2,512,512]{4,3,2,1,0:T(8,128)(2,1)S(1)}, bf16[1,1,2,512,512]{4,3,2,1,0:T(8,128)(2,1)S(1)}, u32[]{:S(2)}, u32[]{:S(2)}) collective-permute-start(bf16[1,1,2,512,512]{4,3,2,1,0:T(8,128)(2,1)S(1)} %get-tuple-element.16), channel_id=1, source_target_pairs={{0,7},{1,0},{2,1},{3,2},{4,3},{5,4},{6,5},{7,6},{8,15},{9,8},{10,9... | collective-permute-start | bytes 3145736 | tf_op jit(solution)/shard_map/ppermute | solution.py:161
  45.2 58.1 %collective-permute-start = (bf16[1,1,512,512]{3,2,1,0:T(8,128)(2,1)S(1)}, bf16[1,1,512,512]{3,2,1,0:T(8,128)(2,1)S(1)}, u32[]{:S(2)}, u32[]{:S(2)}) collective-permute-start(bf16[1,1,512,512]{3,2,1,0:T(8,128)(2,1)S(1)} %get-tuple-element.34), channel_id=1, source_target_pairs={{0,8},{8,16},{16,24},{24,0},{1,9},{9,17},{17,25},{25,1},{2,10},{10... | collective-permute-start | bytes 1572872 | tf_op jit(solution)/shard_map/ppermute | solution.py:161
  47.0 57.8 %collective-permute-start.4 = (bf16[1,1,2,512,512]{4,3,2,1,0:T(8,128)(2,1)S(1)}, bf16[1,1,2,512,512]{4,3,2,1,0:T(8,128)(2,1)S(1)}, u32[]{:S(2)}, u32[]{:S(2)}) collective-permute-start(bf16[1,1,2,512,512]{4,3,2,1,0:T(8,128)(2,1)S(1)} %get-tuple-element.18), channel_id=1, source_target_pairs={{0,1},{1,2},{2,3},{3,4},{4,5},{5,6},{6,7},{7,0},{8,9},{9,10},{10,1... | collective-permute-start | bytes 3145736 | tf_op jit(solution)/shard_map/ppermute | solution.py:161
  104.1 9.6 %collective-permute-start.5 = (bf16[1,1,512,512]{3,2,1,0:T(8,128)(2,1)S(1)}, bf16[1,1,512,512]{3,2,1,0:T(8,128)(2,1)S(1)}, u32[]{:S(2)}, u32[]{:S(2)}) collective-permute-start(bf16[1,1,512,512]{3,2,1,0:T(8,128)(2,1)S(1)} %get-tuple-element.32), channel_id=1, source_target_pairs={{0,7},{1,0},{2,1},{3,2},{4,3},{5,4},{6,5},{7,6},{8,15},{9,8},{10,9... | collective-permute-start | bytes 1572872 | tf_op jit(solution)/shard_map/ppermute | solution.py:161
